TPU v7x, 32 devices: a whole 2x2x4 slice. The times are simulated.
32 devices in a mesh: tmpl: 2 (over core), row: 4 (over z), col: 4 (over y, x).
Axes of the slice: x: 2, y: 2, z: 4, core: 2. Of those that a mesh axis runs over, the one named last changes fastest.
Arguments:
- template_pair: bfloat16 [2, 512, 64, 512], P('tmpl', 'row', None, 'col'), may hold values from -6 to 6
- trunk: bfloat16 [512, 128, 512], P('row', None, 'col'), may hold values from -6 to 6
- coverage: int32 [2, 512], replicated, may hold values from 0 to 1, as said below
- chain_ids: int32 [512], replicated, may hold values from 0 to 3, never falling along the last dimension, each value on 1 to 256 neighbouring positions
- chain_vec: float32 [64], replicated, may hold values from -4 to 4
- trunk_weights: bfloat16 [64, 128], replicated, may hold values from -0.5 to 0.5
- proj_weights: bfloat16 [2, 5, 64, 64], replicated, may hold values from -0.75 to 0.75
- out_weights: bfloat16 [2, 64, 64], replicated, may hold values from -0.75 to 0.75
- final_weights: bfloat16 [128, 64], replicated, may hold values from -0.75 to 0.75
Outputs:
- trunk_out: bfloat16 [512, 128, 512], P('row', None, 'col')
Inputs may be any that keep to these rules, and one draw needn't show every extreme that they name: coverage[t, i] is 1 where template t covers token i, else 0; how densely a template covers tokens is drawn anew for each block of 128 consecutive tokens. `chain_ids`: chain ids never fall along the tokens.
All inputs are finite; a program needn't handle non-finite values.
Results may differ from a plain program's by a relative error of at most 0.008.
Values may be sent and summed in bfloat16 or wider, within the bound.
No kernel may reach another device: no remote copies, remote signals or barrier semaphores. Data moves between devices by JAX's collectives and lax.ppermute only.
A program may use at most 128 MiB of HBM per device.

v0:
```python
import jax
import jax.numpy as jnp
from jax import lax
from jax.sharding import PartitionSpec as P

epsilon = 1e-05


def from_root(block, axis, source):
    block = jnp.where(lax.axis_index(axis) == source, block, jnp.zeros_like(block))
    return lax.psum(block, axis)


def channel_norm(values):
    centre = jnp.mean(values, axis=1, keepdims=True)
    centred = values - centre
    spread = jnp.mean(centred * centred, axis=1, keepdims=True)
    return centred * lax.rsqrt(spread + epsilon)


def project(weights, values):
    return jnp.einsum("dc,icj->idj", weights, values, preferred_element_type=jnp.float32)


def rounded(values):
    return lax.optimization_barrier(values.astype(jnp.bfloat16)).astype(jnp.float32)


def gated_pair(pair_rep, pair_mask, weights):
    channels = pair_rep.shape[1]
    normed = channel_norm(pair_rep.astype(jnp.float32)).astype(jnp.bfloat16)
    stacked = project(weights.reshape(5 * channels, channels), normed)
    pieces = [stacked[:, number * channels : (number + 1) * channels, :] for number in range(5)]
    weighted = pair_mask[:, None, :]
    left_proj = (weighted * jax.nn.sigmoid(pieces[0]) * pieces[1]).astype(jnp.bfloat16)
    right_proj = (weighted * jax.nn.sigmoid(pieces[2]) * pieces[3]).astype(jnp.bfloat16)
    return (left_proj, right_proj, pieces[4])


def apply_update(pair_rep, tri_sum, gate_proj, weights):
    tri_norm = channel_norm(tri_sum).astype(jnp.bfloat16)
    update = jax.nn.sigmoid(gate_proj) * project(weights, tri_norm)
    return (pair_rep.astype(jnp.float32) + update).astype(jnp.bfloat16)


def outgoing(left_proj, right_proj):
    right_cols = lax.all_gather(right_proj, "row", axis=0, tiled=True)
    partial_value = jnp.einsum(
        "ick,jck->icj", left_proj, right_cols, preferred_element_type=jnp.float32
    )
    return lax.psum_scatter(
        partial_value.astype(jnp.bfloat16), "col", scatter_dimension=2, tiled=True
    ).astype(jnp.float32)


def incoming(left_proj, right_proj):
    tile_rows, channels, tile_cols = left_proj.shape
    row_devices = lax.axis_size("row")
    owners = row_devices // lax.axis_size("col")
    left_cols, right_cols = (
        lax.all_gather(left_proj, "row", axis=0, tiled=True),
        lax.all_gather(right_proj, "row", axis=0, tiled=True),
    )
    offset = lax.axis_index("row") % owners * tile_rows
    column_piece = lax.dynamic_slice_in_dim(left_cols, offset, tile_rows, 2)
    left_mine = from_root(column_piece, "col", lax.axis_index("row") // owners)
    left_split = left_mine.reshape(row_devices, tile_rows, channels, tile_rows)
    right_split = right_cols.reshape(row_devices, tile_rows, channels, tile_cols)
    blocks = jnp.einsum(
        "gkci,gkcj->gicj", left_split, right_split, preferred_element_type=jnp.float32
    )
    return jnp.sum(rounded(blocks), axis=0)


def finish(trunk, pooled, cover_count, final_weights):
    hidden = jax.nn.relu(pooled / jnp.maximum(cover_count, 1.0)[:, None, :]).astype(jnp.bfloat16)
    return (trunk.astype(jnp.float32) + project(final_weights, hidden)).astype(jnp.bfloat16)


def per_device(
    template_pair,
    trunk,
    coverage,
    chain_ids,
    chain_vec,
    trunk_weights,
    proj_weights,
    out_weights,
    final_weights,
):
    tile_rows, trunk_channels, tile_cols = trunk.shape
    row_start = lax.axis_index("row") * tile_rows
    col_start = lax.axis_index("col") * tile_cols
    cover_float = coverage.astype(jnp.float32)
    cover_rows = lax.dynamic_slice_in_dim(cover_float, row_start, tile_rows, 1)
    cover_cols = lax.dynamic_slice_in_dim(cover_float, col_start, tile_cols, 1)
    cover_count = jnp.sum(cover_rows[:, :, None] * cover_cols[:, None, :], axis=0)
    chain_rows = lax.dynamic_slice_in_dim(chain_ids, row_start, tile_rows, 0)
    chain_cols = lax.dynamic_slice_in_dim(chain_ids, col_start, tile_cols, 0)
    same_chain = (chain_rows[:, None] == chain_cols[None, :]).astype(jnp.float32)
    trunk_proj = project(trunk_weights, channel_norm(trunk.astype(jnp.float32)))
    local_templates = template_pair.shape[0]
    template_index = lax.axis_index("tmpl") * local_templates + 0
    mask_rows = lax.dynamic_index_in_dim(cover_rows, template_index, 0, keepdims=False)
    mask_cols = lax.dynamic_index_in_dim(cover_cols, template_index, 0, keepdims=False)
    pair_mask = mask_rows[:, None] * mask_cols[None, :]
    pair_rep = (
        template_pair[0].astype(jnp.float32)
        + same_chain[:, None, :] * chain_vec[None, :, None]
        + trunk_proj
    ).astype(jnp.bfloat16)
    left_proj, right_proj, gate_proj = gated_pair(pair_rep, pair_mask, proj_weights[0])
    pair_rep = apply_update(pair_rep, outgoing(left_proj, right_proj), gate_proj, out_weights[0])
    left_proj, right_proj, gate_proj = gated_pair(pair_rep, pair_mask, proj_weights[1])
    pair_rep = apply_update(pair_rep, incoming(left_proj, right_proj), gate_proj, out_weights[1])
    pooled = pair_mask[:, None, :] * channel_norm(pair_rep.astype(jnp.float32))
    pooled_all = lax.psum(pooled.astype(jnp.bfloat16), "tmpl").astype(jnp.float32)
    return finish(trunk, pooled_all, cover_count, final_weights)


def solution(mesh):
    in_specs = (
        P("tmpl", "row", None, "col"),
        P("row", None, "col"),
        P(),
        P(),
        P(),
        P(),
        P(),
        P(),
        P(),
    )
    out_specs = P("row", None, "col")
    return jax.shard_map(
        per_device, mesh=mesh, in_specs=in_specs, out_specs=out_specs, check_vma=False
    )
```

profile of v0, /device:TPU:0, one launch (start us, length us, event | category | flops | bytes accessed | tf_op | source)
XLA Modules:
  0.0 877.5 jit_solution(267695753060939710)
XLA Ops:
  6.5 0.0 all-gather.4.cloned.1.call-start
  6.5 0.8 fusion.84
  7.4 6.4 copy.107
  13.7 3.5 convert_reduce_fusion.2
  17.3 0.0 copy-done.2
  17.3 4.8 fusion.2
  22.1 0.1 compare_convert_fusion
  22.2 0.0 copy-start.8
  22.2 0.0 copy-start.9
  22.2 6.3 convert_reduce_fusion.4
  28.6 0.9 fusion.24
  29.6 8.5 convolution_bitcast_fusion.1
  38.1 0.1 dynamic-slice_bitcast_fusion.1
  38.2 0.1 broadcast_multiply_fusion.6
  38.2 8.4 fusion.47
  46.7 0.0 all-gather.4.cloned.1.call-update
  46.7 0.3 reduce-scatter.2.cloned.1.call-start
  47.0 152.2 %all-gather.4.cloned.1.call-done = bf16[512,64,128]{2,1,0:T(8,128)(2,1)} async-done(((bf16[128,64,128]{2,1,0:T(8,128)(2,1)}), bf16[512,64,128]{2,1,0:T(8,128)(2,1)}) %all-gather.4.cloned.1.call-update) | async-done | bytes 8388624 | tf_op jit(solution)/shard_map/all_gather | solution.py:47
  199.2 15.7 %convert_bitcast_fusion.1 = bf16[128,64,512]{0,2,1:T(8,128)(2,1)} fusion(bf16[512,64,128]{2,1,0:T(8,128)(2,1)} %all-gather.4.cloned.1.call-done, bf16[128,64,128]{2,1,0:T(8,128)(2,1)S(1)} %get-tuple-element.9), kind=kOutput, calls=%fused_computation.17 | convolution fusion | flops 1077936128 | bytes 18874368 | tf_op jit(solution)/shard_map/ick,jck->icj/dot_general | solution.py:48
  214.9 0.0 reduce-scatter.2.cloned.1.call-update
  214.9 0.3 all-gather.8.cloned.1.call-start
  215.2 84.4 %reduce-scatter.2.cloned.1.call-done = bf16[128,64,128]{0,2,1:T(8,128)(2,1)} async-done(((bf16[128,64,512]{0,2,1:T(8,128)(2,1)}), bf16[128,64,128]{0,2,1:T(8,128)(2,1)}) %reduce-scatter.2.cloned.1.call-update) | async-done | bytes 2097168 | tf_op jit(solution)/shard_map/reduce_scatter | solution.py:51
  299.6 2.1 convert_reduce_fusion.6
  301.6 0.1 copy.112
  301.7 0.1 copy.113
  301.8 2.2 fusion.29
  304.0 0.1 copy.114
  304.1 0.1 copy.115
  304.2 0.0 copy-start.11
  304.2 2.0 fusion.30
  306.2 4.3 copy.116
  310.5 4.8 convert_reduce_fusion.3
  315.4 1.0 fusion.22
  316.4 2.9 convolution_bitcast_fusion
  319.3 4.4 fusion.38
  323.7 3.8 copy-done.1
  327.5 0.0 all-gather.8.cloned.1.call-update
  327.5 0.0 all-gather.6.cloned.1.call-start
  327.6 0.5 all-gather.6.cloned.1.call-update
  328.1 0.5 all-reduce.3.cloned.1.call-start
  328.6 148.6 %all-gather.8.cloned.1.call-done = bf16[512,64,128]{2,1,0:T(8,128)(2,1)} async-done(((bf16[128,64,128]{2,1,0:T(8,128)(2,1)}), bf16[512,64,128]{2,1,0:T(8,128)(2,1)}) %all-gather.8.cloned.1.call-update) | async-done | bytes 8388624 | tf_op jit(solution)/shard_map/all_gather | solution.py:61
  477.3 7.4 broadcast_select_fusion
  484.7 12.9 %copy.118 = bf16[4,128,64,128]{3,1,2,0:T(8,128)(2,1)} copy(bf16[4,128,64,128]{3,2,1,0:T(8,128)(2,1)} %bitcast.56) | data formatting | bytes 16777216 | tf_op jit(solution)/shard_map/reshape | solution.py:67
  497.6 0.0 all-reduce.3.cloned.1.call-update
  497.6 0.2 all-reduce.5.cloned.1.call-start
  497.8 128.7 %all-gather.6.cloned.1.call-done = bf16[512,64,128]{2,1,0:T(8,128)(2,1)} async-done(((bf16[128,64,128]{2,1,0:T(8,128)(2,1)}), bf16[512,64,128]{2,1,0:T(8,128)(2,1)}) %all-gather.6.cloned.1.call-update) | async-done | bytes 8388624 | tf_op jit(solution)/shard_map/all_gather | solution.py:62
  626.5 173.6 %all-reduce.3.cloned.1.call-done = bf16[4,128,64,128]{3,1,2,0:T(8,128)(2,1)} async-done(((bf16[4,128,64,128]{3,1,2,0:T(8,128)(2,1)}), bf16[4,128,64,128]{3,1,2,0:T(8,128)(2,1)}) %all-reduce.3.cloned.1.call-update) | async-done | bytes 8388624 | tf_op jit(solution)/shard_map/psum | solution.py:11
  800.2 10.6 %convert_bitcast_fusion = bf16[4,128,64,128]{1,3,2,0:T(8,128)(2,1)S(1)} fusion(bf16[4,128,64,128]{3,1,2,0:T(8,128)(2,1)} %all-reduce.3.cloned.1.call-done, bf16[4,128,64,128]{3,2,1,0:T(8,128)(2,1)} %bitcast.57), kind=kOutput, calls=%fused_computation.16 | convolution fusion | flops 1077936128 | bytes 25165824 | tf_op jit(solution)/shard_map/gkci,gkcj->gicj/dot_general | solution.py:69
  810.7 5.0 convert_reduce_fusion
  815.7 0.1 copy.120
  815.9 0.1 copy.121
  816.0 2.6 multiply_reduce_fusion
  818.6 0.1 copy.122
  818.7 0.1 copy.123
  818.8 4.4 multiply_convert_fusion
  823.2 4.3 copy.124
  827.6 4.8 convert_reduce_fusion.5
  832.4 1.0 fusion.26
  833.4 2.3 fusion.28
  835.7 0.0 all-reduce.5.cloned.1.call-update
  835.7 0.1 multiply_reduce_fusion.1
  835.8 22.0 %all-reduce.5.cloned.1.call-done = bf16[128,64,128]{2,1,0:T(8,128)(2,1)} async-done(((bf16[128,64,128]{2,1,0:T(8,128)(2,1)}), bf16[128,64,128]{2,1,0:T(8,128)(2,1)}) %all-reduce.5.cloned.1.call-update) | async-done | bytes 2097168 | tf_op jit(solution)/shard_map/psum | solution.py:117
  857.8 6.2 fusion.5
  864.1 6.4 copy.125
  (39 shorter events, 0.2 us)
Async XLA Ops:
  6.5 851.3 %copy-start = (bf16[128,64]{0,1:T(8,128)(2,1)S(1)}, bf16[128,64]{0,1:T(8,128)(2,1)}, u32[]{:S(2)}) copy-start(bf16[128,64]{0,1:T(8,128)(2,1)} %param.17) | copy-start | bytes 49156
  6.5 192.7 %all-gather.4.cloned.1.call-start = ((), (), s32[]{:S(2)}) async-start(), calls=%async_computation.1 | async-start | bytes 10485760 | tf_op jit(solution)/shard_map/all_gather | solution.py:47
  13.7 3.5 copy-start.2
  13.7 8.4 copy-start.10
  13.7 8.5 copy-start.12
  13.7 8.5 copy-start.13
  22.2 7.3 copy-start.8
  22.2 7.3 copy-start.9
  28.5 9.5 %copy-start.4 = (bf16[128,64,128]{2,1,0:T(8,128)(2,1)}, bf16[128,64,128]{2,1,0:T(8,128)(2,1)S(1)}, u32[]{:S(2)}) copy-start(bf16[128,64,128]{2,1,0:T(8,128)(2,1)S(1)} %get-tuple-element.20) | copy-start | bytes 6291460
  46.7 252.9 %reduce-scatter.2.cloned.1.call-start = ((), (), s32[]{:S(2)}) async-start(), calls=%async_computation.2 | async-start | bytes 10485760 | tf_op jit(solution)/shard_map/reduce_scatter | solution.py:51
  214.9 262.4 %all-gather.8.cloned.1.call-start = ((), (), s32[]{:S(2)}) async-start(), calls=%async_computation.4 | async-start | bytes 10485760 | tf_op jit(solution)/shard_map/all_gather | solution.py:61
  299.6 4.6 copy-start.3
  304.2 6.3 copy-start.11
  306.2 4.3 copy-start.5
  315.3 3.9 copy-start.6
  319.3 8.2 copy-start.1
  327.5 299.0 %all-gather.6.cloned.1.call-start = ((), (), s32[]{:S(2)}) async-start(), calls=%async_computation.3 | async-start | bytes 10485760 | tf_op jit(solution)/shard_map/all_gather | solution.py:62
  328.1 472.1 %all-reduce.3.cloned.1.call-start = ((), (), s32[]{:S(2)}) async-start(), calls=%async_computation.5 | async-start | bytes 16777216 | tf_op jit(solution)/shard_map/psum | solution.py:11
  497.6 360.2 %all-reduce.5.cloned.1.call-start = ((), (), s32[]{:S(2)}) async-start(), calls=%async_computation.6 | async-start | bytes 4194304 | tf_op jit(solution)/shard_map/psum | solution.py:117
  818.8 8.7 copy-start.7
Sparse Core Ops, SparseCore 0:
  46.8 152.3 all-gather.3
  215.0 84.4 reduce-scatter.1
  327.7 149.5 all-gather.7
  478.7 147.7 all-gather.5
  629.9 170.2 all-reduce.2
  835.8 21.9 all-reduce.4
where the time goes:
time: 884 us; the launch traced here: 878 us
  waiting for transfers between devices  710 us (80%)
  matrix products  59.8 us (7%)
  other arithmetic  52.4 us (6%)
  local copies, waits for them, and re-layouts  39.7 us (4%)
  between operations  14.1 us (2%)
    psum x1, waiting for transfers between devices, from_root(): return lax.psum(block, axis)  174 us
    all_gather x1, waiting for transfers between devices, outgoing(): right_cols = lax.all_gather(right_proj, 'row', axis=0, tiled=True)  152 us
    all_gather x1, waiting for transfers between devices, incoming(): lax.all_gather(left_proj, 'row', axis=0, tiled=True)  149 us
    all_gather x1, waiting for transfers between devices, incoming(): lax.all_gather(right_proj, 'row', axis=0, tiled=True)  129 us
    reduce_scatter x1, waiting for transfers between devices, outgoing(): lax.psum_scatter(partial_value.astype(jnp.bfloat16), 'col', scatter_dimen...  84.4 us
    dot_general x6, matrix products, project(): jnp.einsum('dc,icj->idj', weights, values, preferred_element_type=jnp.flo...  33.5 us
    psum x1, waiting for transfers between devices, per_device(): lax.psum(pooled.astype(jnp.bfloat16), 'tmpl').astype(jnp.float32)  22 us
  transfers between devices with their start and end apart: 6, of which 6 were waited for; matrix products, arithmetic and copies ran while one was open for 2% of the time, Pallas kernels for 0%

commit v1 on v0

v1 whole, which is shorter than its diff:
```python
import functools

import jax
import jax.numpy as jnp
from jax import lax
from jax.experimental import pallas as pl
from jax.experimental.pallas import tpu as pltpu
from jax.sharding import PartitionSpec as P

epsilon = 1e-05
GROUP = 16
F32 = jnp.float32
BF16 = jnp.bfloat16


def sigmoid(x):
    return 0.5 * jnp.tanh(0.5 * x) + 0.5


def norm_rows(x):
    scale = 1.0 / x.shape[0]
    centred = x - jnp.sum(x, axis=0, keepdims=True) * scale
    spread = jnp.sum(centred * centred, axis=0, keepdims=True) * scale
    return centred * lax.rsqrt(spread + epsilon)


def project_rows(weights, rows):
    wide = jnp.concatenate(rows, axis=1)
    out = jnp.dot(weights, wide, preferred_element_type=F32)
    cols = rows[0].shape[1]
    return [out[:, n * cols : (n + 1) * cols] for n in range(len(rows))]


def emit_gated(reps, masks, first, weights_ref, gate_ref, scratch):
    channels = reps[0].shape[0]
    normed = [norm_rows(rep).astype(BF16) for rep in reps]
    for half in range(0, len(reps), 2):
        pieces = project_rows(weights_ref[...], normed[half : half + 2])
        for n, piece in enumerate(pieces):
            p = [piece[k * channels : (k + 1) * channels] for k in range(5)]
            at = first + half + n
            rows = pl.ds(pl.multiple_of(at * channels, channels), channels)
            mask = masks[half + n]
            scratch[0, rows, :] = mask * sigmoid(p[0]) * p[1]
            scratch[1, rows, :] = mask * sigmoid(p[2]) * p[3]
            gate_ref[at] = sigmoid(p[4]).astype(gate_ref.dtype)


def store_by_channel(scratch, pair_ref):
    slots, _, per_slot = pair_ref.shape[:3]
    channels = slots * per_slot
    for side in range(2):
        for channel in range(channels):
            rows = scratch[side, pl.ds(channel, GROUP, stride=channels), :]
            pair_ref[channel // per_slot, side, channel % per_slot] = rows.astype(BF16)


STEP = 4


def pre_kernel(cover_ref, chain_ref, tp_ref, trunk_ref, cover_cols_ref, chain_cols_ref, chain_vec_ref,
               trunk_weights_ref, weights_ref, pair_ref, rep_ref, gate_ref, scratch):
    base = pl.program_id(0) * GROUP
    cols = tp_ref.shape[3]
    channels = tp_ref.shape[2]
    trunk_weights = trunk_weights_ref[...]
    weight_sums = jnp.sum(trunk_weights.astype(F32), axis=1, keepdims=True)

    def body(step, carry):
        first = step * STEP
        reps, masks = [], []
        rows = [trunk_ref[first + n] for n in range(STEP)]
        projected = []
        for half in range(0, STEP, 2):
            projected += project_rows(trunk_weights, rows[half : half + 2])
        for n in range(STEP):
            at = first + n
            values = rows[n].astype(F32)
            scale = 1.0 / values.shape[0]
            centre = jnp.sum(values, axis=0, keepdims=True) * scale
            centred = values - centre
            spread = jnp.sum(centred * centred, axis=0, keepdims=True) * scale
            trunk_proj = (projected[n] - weight_sums * centre) * lax.rsqrt(spread + epsilon)
            same = (chain_cols_ref[...] == chain_ref[base + at]).astype(F32)
            rep = (tp_ref[0, at].astype(F32) + same * chain_vec_ref[...] + trunk_proj).astype(BF16)
            rep_ref[at] = rep
            reps.append(rep.astype(F32))
            masks.append(cover_cols_ref[...] * cover_ref[base + at])
        emit_gated(reps, masks, first, weights_ref, gate_ref, scratch)
        return carry

    lax.fori_loop(0, GROUP // STEP, body, 0)
    store_by_channel(scratch, pair_ref)


def load_tri(tri_ref, tri_scratch):
    channels = tri_ref.shape[0]
    scale = 1.0 / channels
    half = GROUP // 2
    for part in range(2):
        rows = slice(part * half, (part + 1) * half)
        total = jnp.zeros((half, tri_ref.shape[2]), F32)
        for channel in range(channels):
            total += tri_ref[channel].astype(F32)[rows]
        centre = total * scale
        total = jnp.zeros_like(total)
        for channel in range(channels):
            centred = tri_ref[channel].astype(F32)[rows] - centre
            total += centred * centred
        inverse = lax.rsqrt(total * scale + epsilon)
        for channel in range(channels):
            tri_scratch[channel * GROUP + part * half : channel * GROUP + (part + 1) * half, :] = (
                tri_ref[channel].astype(F32)[rows] - centre
            ) * inverse


def updated_rows(first, tri_scratch, rep_ref, gate_ref, out_weights_ref):
    channels = rep_ref.shape[1]
    normed = [
        tri_scratch[pl.ds(first + n, channels, stride=GROUP), :].astype(BF16) for n in range(STEP)
    ]
    projected = []
    for half in range(0, STEP, 2):
        projected += project_rows(out_weights_ref[...], normed[half : half + 2])
    return [
        (rep_ref[first + n].astype(F32) + gate_ref[first + n].astype(F32) * projected[n]).astype(BF16)
        for n in range(STEP)
    ]


def mid_kernel(cover_ref, tri_ref, rep_in_ref, gate_in_ref, cover_cols_ref, out_weights_ref, weights_ref,
               pair_ref, rep_ref, gate_ref, scratch, tri_scratch):
    base = pl.program_id(0) * GROUP
    load_tri(tri_ref, tri_scratch)

    def body(step, carry):
        first = step * STEP
        rows = updated_rows(first, tri_scratch, rep_in_ref, gate_in_ref, out_weights_ref)
        masks = []
        for n in range(STEP):
            rep_ref[first + n] = rows[n]
            masks.append(cover_cols_ref[...] * cover_ref[base + first + n])
        emit_gated([row.astype(F32) for row in rows], masks, first, weights_ref, gate_ref, scratch)
        return carry

    lax.fori_loop(0, GROUP // STEP, body, 0)
    store_by_channel(scratch, pair_ref)


def last_kernel(cover_ref, tri_ref, rep_in_ref, gate_in_ref, cover_cols_ref, out_weights_ref, pooled_ref, tri_scratch):
    base = pl.program_id(0) * GROUP
    load_tri(tri_ref, tri_scratch)

    def body(step, carry):
        first = step * STEP
        rows = updated_rows(first, tri_scratch, rep_in_ref, gate_in_ref, out_weights_ref)
        for n in range(STEP):
            mask = cover_cols_ref[...] * cover_ref[base + first + n]
            pooled_ref[first + n] = (mask * norm_rows(rows[n].astype(F32))).astype(BF16)
        return carry

    lax.fori_loop(0, GROUP // STEP, body, 0)


def finish_kernel(cover_ref, mine_ref, other_ref, trunk_ref, cover_cols_ref, final_weights_ref, out_ref):
    base = pl.program_id(0) * GROUP

    def body(step, carry):
        first = step * STEP
        hidden = []
        for n in range(STEP):
            at = first + n
            count = sum(
                cover_cols_ref[t : t + 1, :] * cover_ref[t, base + at] for t in range(cover_cols_ref.shape[0])
            )
            pooled = mine_ref[at].astype(F32) + other_ref[at].astype(F32)
            hidden.append(jnp.maximum(pooled / jnp.maximum(count, 1.0), 0.0).astype(BF16))
        for half in range(0, STEP, 2):
            for n, row in enumerate(project_rows(final_weights_ref[...], hidden[half : half + 2])):
                at = first + half + n
                out_ref[at] = (trunk_ref[at].astype(F32) + row).astype(BF16)
        return carry

    lax.fori_loop(0, GROUP // STEP, body, 0)


def outgoing_kernel(rows_n, cols_n, pair_ref, tri_ref):
    height = pair_ref.shape[3]
    left = jnp.concatenate(
        [
            jnp.concatenate([pair_ref[r * cols_n + c, 0, 0] for c in range(cols_n)], axis=1)
            for r in range(rows_n)
        ],
        axis=0,
    )
    right = jnp.concatenate(
        [
            jnp.concatenate([pair_ref[r * cols_n + c, 1, 0] for c in range(cols_n)], axis=1)
            for r in range(rows_n)
        ],
        axis=0,
    )
    out = lax.dot_general(left, right, (((1,), (1,)), ((), ())), preferred_element_type=F32)
    width = tri_ref.shape[3]
    for r in range(rows_n):
        for c in range(cols_n):
            tri_ref[r * cols_n + c, 0] = out[
                r * height : (r + 1) * height, c * width : (c + 1) * width
            ].astype(BF16)


def incoming_kernel(rows_n, cols_n, pair_ref, tri_ref):
    left = jnp.concatenate(
        [
            jnp.concatenate([pair_ref[r * cols_n + c, 0, 0] for c in range(cols_n)], axis=1)
            for r in range(rows_n)
        ],
        axis=0,
    )
    right = jnp.concatenate(
        [
            jnp.concatenate([pair_ref[r * cols_n + c, 1, 0] for c in range(cols_n)], axis=1)
            for r in range(rows_n)
        ],
        axis=0,
    )
    out = lax.dot_general(left, right, (((0,), (0,)), ((), ())), preferred_element_type=F32)
    height, width = tri_ref.shape[2:]
    for r in range(rows_n):
        for c in range(cols_n):
            tri_ref[r * cols_n + c, 0] = out[
                r * height : (r + 1) * height, c * width : (c + 1) * width
            ].astype(BF16)


def triangle(body, rows_n, cols_n, pairs, name):
    slots, _, per_slot, height, width = pairs.shape
    return pl.pallas_call(
        functools.partial(body, rows_n, cols_n),
        grid=(per_slot,),
        in_specs=[pl.BlockSpec((slots, 2, 1, height, width), lambda c: (0, 0, c, 0, 0))],
        out_specs=pl.BlockSpec((slots, 1, height, width), lambda c: (0, c, 0, 0)),
        out_shape=jax.ShapeDtypeStruct((slots, per_slot, height, width), BF16),
        name=name,
    )(pairs)


SMEM = pl.BlockSpec(memory_space=pltpu.SMEM)


def whole_block(array):
    zeros = (0,) * array.ndim
    return pl.BlockSpec(array.shape, lambda g: zeros)


def rows_block(*rest):
    zeros = (0,) * len(rest)
    return pl.BlockSpec((GROUP,) + rest, lambda g: (g,) + zeros)


def per_device(
    template_pair,
    trunk,
    coverage,
    chain_ids,
    chain_vec,
    trunk_weights,
    proj_weights,
    out_weights,
    final_weights,
):
    tile_rows, trunk_channels, tile_cols = trunk.shape
    channels = template_pair.shape[2]
    rows_n, cols_n = lax.axis_size("row"), lax.axis_size("col")
    slots = rows_n * cols_n
    per_slot = channels // slots
    grid = (tile_rows // GROUP,)
    row_start = lax.axis_index("row") * tile_rows
    col_start = lax.axis_index("col") * tile_cols
    cover_float = coverage.astype(F32)
    cover_rows = lax.dynamic_slice_in_dim(cover_float, row_start, tile_rows, 1)
    cover_cols = lax.dynamic_slice_in_dim(cover_float, col_start, tile_cols, 1)
    chain_rows = lax.dynamic_slice_in_dim(chain_ids, row_start, tile_rows, 0)
    chain_cols = lax.dynamic_slice_in_dim(chain_ids, col_start, tile_cols, 0)[None]
    template_index = lax.axis_index("tmpl")
    my_rows = lax.dynamic_index_in_dim(cover_rows, template_index, 0, keepdims=False)
    my_cols = lax.dynamic_index_in_dim(cover_cols, template_index, 0, keepdims=True)
    stacked = proj_weights.reshape(2, 5 * channels, channels)

    pair_spec = pl.BlockSpec((slots, 2, per_slot, GROUP, tile_cols), lambda g: (0, 0, 0, g, 0))
    pair_shape = jax.ShapeDtypeStruct((slots, 2, per_slot, tile_rows, tile_cols), BF16)
    rep_spec = rows_block(channels, tile_cols)
    rep_shape = jax.ShapeDtypeStruct((tile_rows, channels, tile_cols), BF16)
    trunk_spec = rows_block(trunk_channels, tile_cols)
    tri_spec = pl.BlockSpec((channels, GROUP, tile_cols), lambda g: (0, g, 0))
    scratch = pltpu.VMEM((2, GROUP * channels, tile_cols), F32)
    tri_scratch = pltpu.VMEM((channels * GROUP, tile_cols), F32)
    gated_outs = dict(
        out_specs=[pair_spec, rep_spec, rep_spec], out_shape=[pair_shape, rep_shape, rep_shape]
    )

    def exchange(values):
        return lax.all_to_all(values, ("row", "col"), 0, 0, tiled=True)

    chain_column = chain_vec[:, None]
    pairs, rep, gate = pl.pallas_call(
        pre_kernel,
        grid=grid,
        in_specs=[
            SMEM,
            SMEM,
            pl.BlockSpec((1, GROUP, channels, tile_cols), lambda g: (0, g, 0, 0)),
            trunk_spec,
            whole_block(my_cols),
            whole_block(chain_cols),
            whole_block(chain_column),
            whole_block(trunk_weights),
            whole_block(stacked[0]),
        ],
        scratch_shapes=[scratch],
        name="pre",
        **gated_outs,
    )(my_rows, chain_rows, template_pair, trunk, my_cols, chain_cols, chain_column, trunk_weights, stacked[0])

    tri = exchange(triangle(outgoing_kernel, rows_n, cols_n, exchange(pairs), "outgoing"))
    pairs, rep, gate = pl.pallas_call(
        mid_kernel,
        grid=grid,
        in_specs=[
            SMEM,
            tri_spec,
            rep_spec,
            rep_spec,
            whole_block(my_cols),
            whole_block(out_weights[0]),
            whole_block(stacked[1]),
        ],
        scratch_shapes=[scratch, tri_scratch],
        name="mid",
        **gated_outs,
    )(
        my_rows,
        tri.reshape(channels, tile_rows, tile_cols),
        rep,
        gate,
        my_cols,
        out_weights[0],
        stacked[1],
    )

    tri = exchange(triangle(incoming_kernel, rows_n, cols_n, exchange(pairs), "incoming"))
    pooled = pl.pallas_call(
        last_kernel,
        grid=grid,
        in_specs=[SMEM, tri_spec, rep_spec, rep_spec, whole_block(my_cols), whole_block(out_weights[1])],
        out_specs=rep_spec,
        out_shape=rep_shape,
        scratch_shapes=[tri_scratch],
        name="last",
    )(my_rows, tri.reshape(channels, tile_rows, tile_cols), rep, gate, my_cols, out_weights[1])

    other = lax.ppermute(pooled, "tmpl", [(0, 1), (1, 0)])
    return pl.pallas_call(
        finish_kernel,
        grid=grid,
        in_specs=[SMEM, rep_spec, rep_spec, trunk_spec, whole_block(cover_cols), whole_block(final_weights)],
        out_specs=trunk_spec,
        out_shape=jax.ShapeDtypeStruct(trunk.shape, BF16),
        name="finish",
    )(cover_rows, pooled, other, trunk, cover_cols, final_weights)


def solution(mesh):
    in_specs = (
        P("tmpl", "row", None, "col"),
        P("row", None, "col"),
        P(),
        P(),
        P(),
        P(),
        P(),
        P(),
        P(),
    )
    out_specs = P("row", None, "col")
    return jax.shard_map(
        per_device, mesh=mesh, in_specs=in_specs, out_specs=out_specs, check_vma=False
    )
```

time: 884 us -> 395 us (0.45)
  waiting for transfers between devices: 710 us -> 45 us
  blocking collectives: 0 us -> 258 us
  Pallas kernels: 0 us -> 77.1 us
  matrix products: 59.8 us -> 0 us
  other arithmetic: 52.4 us -> 0.69 us
  local copies, waits for them, and re-layouts: 39.7 us -> 9.57 us
  between operations: 14.1 us -> 0.03 us
    all_gather x3 -> x0, waiting for transfers between devices: 430 us -> none  [the longest x1 152 us: outgoing(): right_cols = lax.all_gather(right_proj, 'row', axis=0, tiled=True)]
    all_to_all x0 -> x3, blocking collectives: none -> 258 us  [exchange(): return lax.all_to_all(values, ('row', 'col'), 0, 0, tiled=True)]
    psum x2 -> x0, waiting for transfers between devices: 196 us -> none  [the longest x1 174 us: from_root(): return lax.psum(block, axis)]
    reduce_scatter x1 -> x0, waiting for transfers between devices: 84.4 us -> none  [outgoing(): lax.psum_scatter(partial_value.astype(jnp.bfloat16), 'col', scatter_dimen...]
    pallas_call x0 -> x6, Pallas kernels: none -> 77.1 us  [the longest x1 23.3 us: per_device(): pl.pallas_call(mid_kernel, grid=grid, in_specs=[SMEM, tri_spec, rep_spec,...]
    dot_general x8 -> x0, matrix products: 59.8 us -> none  [the longest x6 33.5 us: project(): jnp.einsum('dc,icj->idj', weights, values, preferred_element_type=jnp.flo...]
    all_to_all x0 -> x1, waiting for transfers between devices: none -> 41.9 us  [exchange(): return lax.all_to_all(values, ('row', 'col'), 0, 0, tiled=True)]
    reduce_sum x10 -> x0, other arithmetic: 23.1 us -> none  [the longest x6 12.5 us: channel_norm(): spread = jnp.mean(centred * centred, axis=1, keepdims=True)]
  transfers between devices with their start and end apart: 6 -> 2, of which waited for: 6 -> 2; matrix products, arithmetic and copies ran while one was open for 2% -> 0% of each run, Pallas kernels for 0% -> 0%
where the time goes in v1:
time: 395 us; the launch traced here: 394 us
  blocking collectives  258 us (65%)
  Pallas kernels  77.1 us (20%)
  waiting for transfers between devices  45 us (11%)
  local copies, waits for them, and re-layouts  9.57 us (2%)
  starting transfers between devices  4.08 us (1%)
    all_to_all x3, blocking collectives, exchange(): return lax.all_to_all(values, ('row', 'col'), 0, 0, tiled=True)  258 us
    all_to_all x1, waiting for transfers between devices, exchange(): return lax.all_to_all(values, ('row', 'col'), 0, 0, tiled=True)  41.9 us
    pallas_call x1, Pallas kernels, per_device(): pl.pallas_call(mid_kernel, grid=grid, in_specs=[SMEM, tri_spec, rep_spec,...  23.3 us
    pallas_call x1, Pallas kernels, per_device(): pl.pallas_call(pre_kernel, grid=grid, in_specs=[SMEM, SMEM, pl.BlockSpec(...  22.1 us
    pallas_call x1, Pallas kernels, per_device(): pl.pallas_call(last_kernel, grid=grid, in_specs=[SMEM, tri_spec, rep_spec...  11.2 us
    pallas_call x1, Pallas kernels, per_device(): pl.pallas_call(finish_kernel, grid=grid, in_specs=[SMEM, rep_spec, rep_sp...  10.4 us
    pallas_call x2, Pallas kernels, triangle(): pl.pallas_call(functools.partial(body, rows_n, cols_n), grid=(per_slot,),...  10.1 us
  transfers between devices with their start and end apart: 2, of which 2 were waited for; matrix products, arithmetic and copies ran while one was open for 0% of the time, Pallas kernels for 0%

profile of v1, /device:TPU:0, one launch (start us, length us, event | category | flops | bytes accessed | tf_op | source)
XLA Modules:
  0.0 394.1 jit_solution(13239378435714392760)
XLA Ops:
  0.0 0.7 convert_element_type.3
  0.7 1.4 dynamic-slice_bitcast_fusion
  2.1 1.4 copy.10.chain_vec_ref
  3.4 1.6 fusion
  5.0 0.6 fusion.1
  5.6 22.1 %pre.1 = (bf16[16,2,4,128,128]{4,3,2,1,0:T(8,128)(2,1)}, bf16[128,64,128]{2,1,0:T(8,128)(2,1)}, bf16[128,64,128]{2,1,0:T(8,128)(2,1)}) custom-call(f32[128]{0:T(128)} %get-tuple-element.24.cover_ref, s32[128]{0:T(128)} %get-tuple-element.26.chain_ref, bf16[1,128,64,128]{3,2,1,0:T(8,128)(2,1)} %tp_ref.1, bf16[128,128,128]{2,1,0:T(8,128)(2,1)} %trunk_ref.3, ...), custom_call_target="tpu_custom_call" | custom-call | tf_op jit(solution)/shard_map/pre/pallas_call | solution.py:306
  27.7 102.2 %all_to_all.20.pair_ref = bf16[16,2,4,128,128]{4,3,2,1,0:T(8,128)(2,1)} all-to-all(bf16[16,2,4,128,128]{4,3,2,1,0:T(8,128)(2,1)} %get-tuple-element.11), channel_id=1, replica_groups=mesh['tmpl'=2,'row'=4,'col'=4] {'row','col'}, dimensions={0} | all-to-all | bytes 8388608 | tf_op jit(solution)/shard_map/all_to_all | solution.py:303
  129.9 5.1 %outgoing.1 = bf16[16,4,128,128]{3,2,1,0:T(8,128)(2,1)} custom-call(bf16[16,2,4,128,128]{4,3,2,1,0:T(8,128)(2,1)} %all_to_all.20.pair_ref), custom_call_target="tpu_custom_call" | custom-call | tf_op jit(solution)/shard_map/outgoing/pallas_call | solution.py:238
  135.0 0.0 copy-start.2
  135.0 4.1 %all-to-all-start.1 = ((bf16[16,4,128,128]{3,2,1,0:T(8,128)(2,1)}), bf16[16,4,128,128]{3,2,1,0:T(8,128)(2,1)S(1)}, u32[]{:S(2)}, u32[]{:S(2)}) async-start(bf16[16,4,128,128]{3,2,1,0:T(8,128)(2,1)} %outgoing.1), calls=%async_computation.1 | async-start | bytes 4194304 | tf_op jit(solution)/shard_map/all_to_all | solution.py:303
  139.1 0.0 copy-done.2
  139.1 0.6 slice_bitcast_fusion
  139.7 41.9 %all-to-all-done.1 = bf16[16,4,128,128]{3,2,1,0:T(8,128)(2,1)S(1)} async-done(((bf16[16,4,128,128]{3,2,1,0:T(8,128)(2,1)}), bf16[16,4,128,128]{3,2,1,0:T(8,128)(2,1)S(1)}, u32[]{:S(2)}, u32[]{:S(2)}) %all-to-all-start.1) | async-done | bytes 2097184 | tf_op jit(solution)/shard_map/all_to_all | solution.py:303
  181.6 0.0 copy-start
  181.6 1.4 copy-done
  183.0 23.3 %mid.1 = (bf16[16,2,4,128,128]{4,3,2,1,0:T(8,128)(2,1)}, bf16[128,64,128]{2,1,0:T(8,128)(2,1)}, bf16[128,64,128]{2,1,0:T(8,128)(2,1)}) custom-call(f32[128]{0:T(128)} %get-tuple-element.24.cover_ref, bf16[64,128,128]{2,1,0:T(8,128)(2,1)} %bitcast.14, bf16[128,64,128]{2,1,0:T(8,128)(2,1)} %get-tuple-element.12.rep_in_ref, ...), custom_call_target="tpu_custom_call" | custom-call | tf_op jit(solution)/shard_map/mid/pallas_call | solution.py:326
  206.3 103.2 %all_to_all.21.pair_ref = bf16[16,2,4,128,128]{4,3,2,1,0:T(8,128)(2,1)} all-to-all(bf16[16,2,4,128,128]{4,3,2,1,0:T(8,128)(2,1)} %get-tuple-element.14), channel_id=1, replica_groups=mesh['tmpl'=2,'row'=4,'col'=4] {'row','col'}, dimensions={0} | all-to-all | bytes 8388608 | tf_op jit(solution)/shard_map/all_to_all | solution.py:303
  309.5 5.0 %incoming.1 = bf16[16,4,128,128]{3,2,1,0:T(8,128)(2,1)} custom-call(bf16[16,2,4,128,128]{4,3,2,1,0:T(8,128)(2,1)} %all_to_all.21.pair_ref), custom_call_target="tpu_custom_call" | custom-call | tf_op jit(solution)/shard_map/incoming/pallas_call | solution.py:238
  314.5 52.3 %all_to_all.22 = bf16[16,4,128,128]{3,2,1,0:T(8,128)(2,1)} all-to-all(bf16[16,4,128,128]{3,2,1,0:T(8,128)(2,1)} %incoming.1), channel_id=1, replica_groups=mesh['tmpl'=2,'row'=4,'col'=4] {'row','col'}, dimensions={0} | all-to-all | bytes 4194304 | tf_op jit(solution)/shard_map/all_to_all | solution.py:303
  366.8 0.0 copy-start.3
  366.8 11.2 %last.1.mine_ref = bf16[128,64,128]{2,1,0:T(8,128)(2,1)} custom-call(f32[128]{0:T(128)} %get-tuple-element.24.cover_ref, bf16[64,128,128]{2,1,0:T(8,128)(2,1)} %bitcast.13, bf16[128,64,128]{2,1,0:T(8,128)(2,1)} %get-tuple-element.15.rep_in_ref, bf16[128,64,128]{2,1,0:T(8,128)(2,1)} %get-tuple-element.16.gate_in_ref, ...), custom_call_target="tpu_custom_call" | custom-call | tf_op jit(solution)/shard_map/last/pallas_call | solution.py:352
  378.0 0.0 collective-permute-start
  378.0 0.0 copy-done.3
  378.0 0.7 copy.11.final_weights_ref
  378.7 0.6 constant_dynamic-slice_fusion
  379.3 3.1 collective-permute-done.other_ref
  382.4 0.0 copy-start.1
  382.4 1.3 copy-done.1
  383.7 10.4 %finish.1 = bf16[128,128,128]{2,1,0:T(8,128)(2,1)} custom-call(f32[2,128]{1,0:T(2,128)} %get-tuple-element.22.cover_ref, bf16[128,64,128]{2,1,0:T(8,128)(2,1)} %last.1.mine_ref, bf16[128,64,128]{2,1,0:T(8,128)(2,1)} %copy-done.1, bf16[128,128,128]{2,1,0:T(8,128)(2,1)} %trunk_ref.3, f32[2,128]{1,0:T(2,128)} %get-tuple-element.21.cover_cols_ref, ...), custom_call_target="tpu_custom_call" | custom-call | tf_op jit(solution)/shard_map/finish/pallas_call | solution.py:363
Async XLA Ops:
  135.0 4.1 %copy-start.2 = (bf16[2,64,64]{2,1,0:T(8,128)(2,1)S(1)}, bf16[2,64,64]{2,1,0:T(8,128)(2,1)}, u32[]{:S(2)}) copy-start(bf16[2,64,64]{2,1,0:T(8,128)(2,1)} %param.16) | copy-start | bytes 49156
  135.0 46.7 %all-to-all-start.1 = ((bf16[16,4,128,128]{3,2,1,0:T(8,128)(2,1)}), bf16[16,4,128,128]{3,2,1,0:T(8,128)(2,1)S(1)}, u32[]{:S(2)}, u32[]{:S(2)}) async-start(bf16[16,4,128,128]{3,2,1,0:T(8,128)(2,1)} %outgoing.1), calls=%async_computation.1 | async-start | bytes 4194304 | tf_op jit(solution)/shard_map/all_to_all | solution.py:303
  181.6 1.4 copy-start
  366.8 11.2 %copy-start.3 = (bf16[128,64]{0,1:T(8,128)(2,1)S(1)}, bf16[128,64]{0,1:T(8,128)(2,1)}, u32[]{:S(2)}) copy-start(bf16[128,64]{0,1:T(8,128)(2,1)} %param.17) | copy-start | bytes 49156
  378.0 4.4 %collective-permute-start = (bf16[128,64,128]{2,1,0:T(8,128)(2,1)}, bf16[128,64,128]{2,1,0:T(8,128)(2,1)S(1)}, u32[]{:S(2)}, u32[]{:S(2)}) collective-permute-start(bf16[128,64,128]{2,1,0:T(8,128)(2,1)} %last.1.mine_ref), channel_id=1, source_target_pairs={{0,16},{16,0},{1,17},{17,1},{2,18},{18,2},{3,19},{19,3},{4,20},{20... | collective-permute-start | bytes 6291464 | tf_op jit(solution)/shard_map/ppermute | solution.py:362
  382.4 1.3 copy-start.1
